TPU v7x, 32 devices: a whole 2x2x4 slice. The times are simulated.
32 devices in a mesh: expert: 2 (over x), dp: 16 (over z, y, core).
Axes of the slice: x: 2, y: 2, z: 4, core: 2. Of those that a mesh axis runs over, the one named last changes fastest.
Arguments:
- features: bfloat16 [4096, 512], P(('expert', 'dp')), may hold values from -31 to 31
- gradients: bfloat16 [4096, 512], P(('expert', 'dp')), may hold values from -31 to 31
- route_ids: int32 [4096, 2], P(('expert', 'dp')), may hold values from 0 to 7, all different within a row; in each aligned block of 128 rows (0 to 127, 128 to 255, ...) at most 64 rows name the same one
- gate_share: float32 [4096], P(('expert', 'dp')), may hold values from 0.5 to 0.95
- token_mask: int32 [4096], P(('expert', 'dp')), may hold values 0 or 1
- damping: float32 [8, 2, 1], P('expert'), may hold values from 0.5 to 2
Outputs:
- act_inverse: float32 [8, 1, 512, 512], P(None, None, 'dp')
- grad_inverse: float32 [8, 1, 512, 512], P(None, None, 'dp')
Inputs may be any that keep to these rules, and one draw needn't show every extreme that they name: `route_ids`: each token names two different experts. Among the 128 tokens of one device no expert is named by more than 64 tokens, a bound that some block reaches.
All inputs are finite; a program needn't handle non-finite values. Where the computation divides by a largest or mean magnitude, that divisor is 1e-20 or more. No bound on the sum of `token_mask` on one device may be relied on, other than what follows from the above.
Results may differ from a plain program's by a relative error of at most 0.0003.
Values may be sent and summed in bfloat16 or wider, within the bound.
No kernel may reach another device: no remote copies, remote signals or barrier semaphores. Data moves between devices by JAX's collectives and lax.ppermute only.
A program may use at most 64 MiB of HBM per device.

v0:
```python
import jax
import jax.numpy as jnp
from jax import lax
from jax.sharding import PartitionSpec as P

EXPERTS = 8
TOP = 2
BLOCK = 512
NBLK = 1
CAP = 64
WIDTH = 512


def slot_table(route_ids, capacity):
    pair_experts = route_ids.reshape(-1)
    onehot = (pair_experts[:, None] == jnp.arange(EXPERTS, dtype=jnp.int32)[None, :]).astype(
        jnp.int32
    )
    running = jnp.cumsum(onehot, axis=0)
    position = jnp.sum(onehot * running, axis=1) - 1
    target = pair_experts * capacity + position
    sources = jnp.arange(1, pair_experts.shape[0] + 1, dtype=jnp.int32)
    return jnp.zeros((EXPERTS * capacity,), jnp.int32).at[target].set(sources)


def newton_rows(rows_now, matrix, whole_now):
    left_product = jnp.einsum("eirk,eikc->eirc", rows_now, matrix, precision=lax.Precision.HIGHEST)
    return 2.0 * rows_now - jnp.einsum(
        "eirk,eikc->eirc", left_product, whole_now, precision=lax.Precision.HIGHEST
    )


def first_iterate(matrix, identity, inverse_bound):
    bound_scale = inverse_bound[:, :, None, None]
    return 2.0 * bound_scale * identity - bound_scale * bound_scale * matrix


def on_device(features, gradients, route_ids, gate_share, token_mask, damping):
    tokens_here = features.shape[0]
    capacity = CAP
    blocks = 2 * NBLK
    kept_mask = token_mask.astype(jnp.float32)
    weight_pair = jnp.stack([gate_share, 1.0 - gate_share], axis=1) * kept_mask[:, None]
    kept_rows = features * token_mask.astype(jnp.bfloat16)[:, None]
    pair_grads = (gradients[:, None, :].astype(jnp.float32) * weight_pair[:, :, None]).astype(
        jnp.bfloat16
    )
    repeated = jnp.broadcast_to(kept_rows[:, None, :], pair_grads.shape)
    pair_rows = jnp.concatenate([repeated, pair_grads], axis=2).reshape(
        tokens_here * TOP, 2 * WIDTH
    )
    padded = jnp.concatenate([jnp.zeros((1, 2 * WIDTH), jnp.bfloat16), pair_rows], axis=0)
    buffer = jnp.take(padded, slot_table(route_ids, capacity), axis=0).reshape(
        EXPERTS, capacity, blocks, BLOCK
    )
    load_inverse = 1.0 / (
        tokens_here * lax.axis_size("expert") * lax.axis_size("dp") * TOP / EXPERTS
    )
    received = lax.all_to_all(buffer, "expert", split_axis=0, concat_axis=1, tiled=True)
    gram_blocks = (
        jnp.einsum("erib,eric->eibc", received, received, preferred_element_type=jnp.float32)
        * load_inverse
    )
    damping_flat = damping.reshape(damping.shape[0], blocks)[:, :, None, None]
    rows_share = BLOCK // lax.axis_size("dp")
    row_start = lax.axis_index("dp") * rows_share
    identity = jnp.eye(BLOCK, dtype=jnp.float32)
    summed = lax.psum(gram_blocks, "dp")
    matrix = summed + damping_flat * identity
    largest_sum = jnp.max(jnp.sum(jnp.abs(matrix), axis=3), axis=2)
    inverse_bound = 1.0 / largest_sum
    iterate_one = first_iterate(matrix, identity, inverse_bound)
    iterate_two = newton_rows(iterate_one, matrix, iterate_one)
    second_rows = lax.dynamic_slice_in_dim(iterate_two, row_start, rows_share, 2)
    third_rows = newton_rows(second_rows, matrix, iterate_two)
    act_rows = third_rows[:, :NBLK]
    grad_rows = third_rows[:, NBLK:]
    act_inverse, grad_inverse = (
        lax.all_gather(act_rows, "expert", axis=0, tiled=True),
        lax.all_gather(grad_rows, "expert", axis=0, tiled=True),
    )
    return (act_inverse, grad_inverse)


def solution(mesh):
    placed = (
        P(("expert", "dp"), None),
        P(("expert", "dp"), None),
        P(("expert", "dp"), None),
        P(("expert", "dp")),
        P(("expert", "dp")),
        P("expert", None, None),
    )
    return jax.shard_map(
        on_device,
        mesh=mesh,
        in_specs=placed,
        out_specs=(P(None, None, "dp", None), P(None, None, "dp", None)),
        check_vma=False,
    )
```

profile of v0, /device:TPU:0, one launch (start us, length us, event | category | flops | bytes accessed | tf_op | source)
XLA Modules:
  0.0 298.0 jit_solution(7920612828320791945)
XLA Ops:
  7.2 0.8 copy.37
  8.0 0.1 eq.38
  8.1 0.1 eq.34
  8.3 0.7 broadcast_multiply_fusion.3
  9.0 0.6 reduce-window.6
  9.6 0.2 slice_reduce_fusion
  10.0 0.1 mul.132
  10.2 1.4 scatter_custom_fusion
  11.6 0.7 fusion.25
  12.4 0.1 mul.139
  12.6 0.7 subtract_bitcast_fusion
  13.2 0.7 pad_maximum_fusion
  14.0 0.1 stack.14
  14.2 1.0 mul.136
  15.2 0.4 mul.137
  15.6 1.0 broadcast_multiply_fusion.1
  16.6 0.1 broadcast_in_dim.36
  17.1 2.1 gather_fusion
  19.2 0.8 gather.7
  20.0 0.2 copy_select_fusion
  20.2 17.7 %all_to_all.18 = bf16[8,64,2,512]{3,1,2,0:T(8,128)(2,1)S(1)} all-to-all(bf16[8,64,2,512]{3,1,2,0:T(8,128)(2,1)S(1)} %copy_select_fusion), channel_id=1, replica_groups=mesh['expert'=2,'dp'=16] {'expert'}, dimensions={0} | all-to-all | bytes 2097152 | tf_op jit(solution)/shard_map/all_to_all | solution.py:59
  38.1 4.5 %broadcast_multiply_fusion = f32[4,2,512,512]{3,2,1,0:T(8,128)} fusion(bf16[4,128,2,512]{3,1,2,0:T(8,128)(2,1)S(1)} %bitcast.23), kind=kOutput, calls=%fused_computation.19 | convolution fusion | flops 538968064 | bytes 9437184 | tf_op jit(solution)/shard_map/erib,eric->eibc/dot_general | solution.py:61
  42.8 170.4 %all-reduce.3.cloned.1.call-done = f32[4,2,512,512]{3,2,1,0:T(8,128)} async-done(((f32[4,2,512,512]{3,2,1,0:T(8,128)}), f32[4,2,512,512]{3,2,1,0:T(8,128)}) %all-reduce.3.cloned.1.call-update) | async-done | bytes 8388624 | tf_op jit(solution)/shard_map/psum | solution.py:68
  213.2 4.6 %abs_reduce_fusion = f32[4,2,512]{2,1,0:T(2,128)S(1)} fusion(f32[4,2,512,512]{3,2,1,0:T(8,128)} %all-reduce.3.cloned.1.call-done, f32[512,512]{1,0:T(8,128)S(1)} %fusion.15, f32[4,2]{1,0:T(4,128)S(1)} %copy.43), kind=kLoop, calls=%fused_computation.6 | loop fusion | flops 8384512 | bytes 9453600 | tf_op jit(solution)/shard_map/reduce_sum | solution.py:70
  218.2 23.3 %fusion.1 = f32[4,2,512,512]{3,2,1,0:T(8,128)} fusion(f32[4,2,512,512]{3,2,1,0:T(8,128)} %all-reduce.3.cloned.1.call-done, f32[4,2]{1,0:T(4,128)S(1)} %copy.46, f32[4,2]{1,0:T(4,128)S(1)} %copy.45, f32[512,512]{1,0:T(8,128)S(1)} %fusion.15, f32[4,2]{1,0:T(4,128)S(1)} %copy.43), kind=kOutput, calls=%fused_computation.5 | convolution fusion | flops 12899581952 | bytes 17825888 | tf_op jit(solution)/shard_map/eirk,eikc->eirc/dot_general | solution.py:27
  241.5 19.9 %multiply_subtract_fusion = f32[4,2,512,512]{3,2,1,0:T(8,128)} fusion(f32[4,2,512,512]{3,2,1,0:T(8,128)} %fusion.1, f32[4,2,512,512]{3,2,1,0:T(8,128)S(1)} %copy-done, f32[4,2]{1,0:T(4,128)S(1)} %copy.46, f32[4,2]{1,0:T(4,128)S(1)} %copy.45, f32[512,512]{1,0:T(8,128)S(1)} %fusion.15, f32[4,2]{1,0:T(4,128)S(1)} %copy.43), kind=kOutput, calls=%fused_computation.2 | convolution fusion | flops 12910067712 | bytes 26214496 | tf_op jit(solution)/shard_map/eirk,eikc->eirc/dot_general | solution.py:28
  261.4 6.8 %fusion.2 = f32[4,2,32,512]{3,2,1,0:T(8,128)S(1)} fusion(f32[4,2,512,512]{3,2,1,0:T(8,128)S(1)} %copy-done, f32[512,512]{1,0:T(8,128)S(1)} %fusion.15, f32[4,2]{1,0:T(4,128)S(1)} %copy.43, f32[4,2,512,512]{3,2,1,0:T(8,128)} %multiply_subtract_fusion, s32[]{:T(128)S(6)} %select_n.26), kind=kOutput, calls=%fused_computation.8 | convolution fusion | flops 809500672 | bytes 10485796 | tf_op jit(solution)/shard_map/eirk,eikc->eirc/dot_general | solution.py:27
  268.2 4.9 %convolution_subtract_fusion = f32[4,2,32,512]{3,2,1,0:T(8,128)S(1)} fusion(f32[4,2,32,512]{3,2,1,0:T(8,128)S(1)} %fusion.2, f32[4,2,512,512]{3,2,1,0:T(8,128)S(1)} %copy-done.1, s32[]{:T(128)S(6)} %select_n.26), kind=kOutput, calls=%fused_computation.20 | convolution fusion | flops 805568512 | bytes 9961476 | tf_op jit(solution)/shard_map/eirk,eikc->eirc/dot_general | solution.py:28
  273.1 8.7 %all_gather.6 = f32[8,1,32,512]{3,2,1,0:T(8,128)S(1)} all-gather(f32[4,1,32,512]{3,2,1,0:T(8,128)S(1)} %get-tuple-element.3), channel_id=1, replica_groups=mesh['expert'=2,'dp'=16] {'expert'}, dimensions={0}, use_global_device_ids=true | all-gather | bytes 786432 | tf_op jit(solution)/shard_map/all_gather | solution.py:79
  281.8 7.8 %all_gather.7 = f32[8,1,32,512]{3,2,1,0:T(8,128)S(1)} all-gather(f32[4,1,32,512]{3,2,1,0:T(8,128)S(1)} %get-tuple-element.2), channel_id=1, replica_groups=mesh['expert'=2,'dp'=16] {'expert'}, dimensions={0}, use_global_device_ids=true | all-gather | bytes 786432 | tf_op jit(solution)/shard_map/all_gather | solution.py:80
  289.6 0.8 copy.53
  290.4 0.8 copy.54
  (35 shorter events, 1.7 us)
Async XLA Ops:
  7.2 206.0 %all-reduce.3.cloned.1.call-start = ((), (), s32[]{:S(2)}) async-start(), calls=%async_computation.1 | async-start | bytes 16777216 | tf_op jit(solution)/shard_map/psum | solution.py:68
  38.1 4.5 %copy-start.2 = (f32[4,2,1]{0,2,1:T(1,128)S(1)}, f32[4,2,1]{0,2,1:T(1,128)}, u32[]{:S(2)}) copy-start(f32[4,2,1]{0,2,1:T(1,128)} %param.11) | copy-start | bytes 100
  218.2 23.3 %copy-start = (f32[4,2,512,512]{3,2,1,0:T(8,128)S(1)}, f32[4,2,512,512]{3,2,1,0:T(8,128)}, u32[]{:S(2)}) copy-start(f32[4,2,512,512]{3,2,1,0:T(8,128)} %all-reduce.3.cloned.1.call-done) | copy-start | bytes 25165828
  261.4 6.8 %copy-start.1 = (f32[4,2,512,512]{3,2,1,0:T(8,128)S(1)}, f32[4,2,512,512]{3,2,1,0:T(8,128)}, u32[]{:S(2)}) copy-start(f32[4,2,512,512]{3,2,1,0:T(8,128)} %multiply_subtract_fusion) | copy-start | bytes 25165828
Sparse Core Ops, SparseCore 0:
  42.7 170.4 all-reduce.2
where the time goes:
time: 298 us
  waiting for transfers between devices  170 us (57%)
  matrix products  59.3 us (20%)
  blocking collectives  34.2 us (11%)
  between operations  14.2 us (5%)
  local copies, waits for them, and re-layouts  10.1 us (3%)
  other arithmetic  9.73 us (3%)
    psum x1, waiting for transfers between devices, on_device(): summed = lax.psum(gram_blocks, 'dp')  170 us
    dot_general x2, matrix products, newton_rows(): jnp.einsum('eirk,eikc->eirc', rows_now, matrix, precision=lax.Precision.H...  30.1 us
    dot_general x2, matrix products, newton_rows(): jnp.einsum('eirk,eikc->eirc', left_product, whole_now, precision=lax.Prec...  24.7 us
    all_to_all x1, blocking collectives, on_device(): lax.all_to_all(buffer, 'expert', split_axis=0, concat_axis=1, tiled=True)  17.7 us
    all_gather x1, blocking collectives, on_device(): lax.all_gather(act_rows, 'expert', axis=0, tiled=True)  8.67 us
    all_gather x1, blocking collectives, on_device(): lax.all_gather(grad_rows, 'expert', axis=0, tiled=True)  7.79 us
  transfers between devices with their start and end apart: 1, of which 1 were waited for; matrix products, arithmetic and copies ran while one was open for 0% of the time, Pallas kernels for 0%

commit v1 on v0

--- a/solution.py
+++ b/solution.py
@@ -65,7 +65,9 @@
     rows_share = BLOCK // lax.axis_size("dp")
     row_start = lax.axis_index("dp") * rows_share
     identity = jnp.eye(BLOCK, dtype=jnp.float32)
-    summed = lax.psum(gram_blocks, "dp")
+    summed = gram_blocks
+    for hop in (1, 2, 4, 8):
+        summed = summed + lax.ppermute(summed, "dp", [(dev, dev ^ hop) for dev in range(16)])
     matrix = summed + damping_flat * identity
     largest_sum = jnp.max(jnp.sum(jnp.abs(matrix), axis=3), axis=2)
     inverse_bound = 1.0 / largest_sum

time: 298 us -> 889 us (2.98)
  waiting for transfers between devices: 170 us -> 734 us
  other arithmetic: 9.73 us -> 48.8 us
  between operations: 14.2 us -> 0.84 us
    ppermute x0 -> x4, waiting for transfers between devices: none -> 734 us  [on_device(): lax.ppermute(summed, 'dp', [(dev, dev ^ hop) for dev in range(16)])]
    psum x1 -> x0, waiting for transfers between devices: 170 us -> none  [on_device(): summed = lax.psum(gram_blocks, 'dp')]
    add x0 -> x3, other arithmetic: none -> 33.2 us  [on_device(): summed + lax.ppermute(summed, 'dp', [(dev, dev ^ hop) for dev in range(16)])]
  transfers between devices with their start and end apart: 1 -> 4, of which waited for: 1 -> 4; matrix products, arithmetic and copies ran while one was open for 0% -> 0% of each run, Pallas kernels for 0% -> 0%
where the time goes in v1:
time: 889 us
  waiting for transfers between devices  734 us (83%)
  matrix products  53.6 us (6%)
  other arithmetic  48.8 us (5%)
  blocking collectives  32.6 us (4%)
  local copies, waits for them, and re-layouts  13.3 us (1%)
    ppermute x4, waiting for transfers between devices, on_device(): lax.ppermute(summed, 'dp', [(dev, dev ^ hop) for dev in range(16)])  734 us
    add x3, other arithmetic, on_device(): summed + lax.ppermute(summed, 'dp', [(dev, dev ^ hop) for dev in range(16)])  33.2 us
    dot_general x2, matrix products, newton_rows(): jnp.einsum('eirk,eikc->eirc', rows_now, matrix, precision=lax.Precision.H...  28.3 us
    dot_general x2, matrix products, newton_rows(): jnp.einsum('eirk,eikc->eirc', left_product, whole_now, precision=lax.Prec...  24 us
  transfers between devices with their start and end apart: 4, of which 4 were waited for; matrix products, arithmetic and copies ran while one was open for 0% of the time, Pallas kernels for 0%

profile of v1, /device:TPU:0, one launch (start us, length us, event | category | flops | bytes accessed | tf_op | source)
XLA Modules:
  0.0 888.7 jit_solution(6632500211606088601)
XLA Ops:
  0.6 0.8 copy.37
  1.7 0.7 broadcast_multiply_fusion.3
  3.6 1.4 scatter_custom_fusion
  5.0 0.7 fusion.21
  6.0 0.7 subtract_bitcast_fusion
  6.7 0.7 pad_maximum_fusion
  7.6 1.0 mul.136
  9.0 1.0 broadcast_multiply_fusion.1
  10.5 2.1 gather_fusion
  12.6 0.8 gather.7
  13.7 17.7 %all_to_all.18 = bf16[8,64,2,512]{3,1,2,0:T(8,128)(2,1)S(1)} all-to-all(bf16[8,64,2,512]{3,1,2,0:T(8,128)(2,1)S(1)} %copy_select_fusion), channel_id=1, replica_groups=mesh['expert'=2,'dp'=16] {'expert'}, dimensions={0} | all-to-all | bytes 2097152 | tf_op jit(solution)/shard_map/all_to_all | solution.py:59
  31.5 1.3 broadcast_multiply_fusion
  32.8 3.2 copy-done.2
  36.0 13.3 %collective-permute-done = f32[4,2,512,512]{3,2,1,0:T(8,128)} collective-permute-done((f32[4,2,512,512]{3,2,1,0:T(8,128)S(1)}, f32[4,2,512,512]{3,2,1,0:T(8,128)}, u32[]{:S(2)}, u32[]{:S(2)}) %collective-permute-start) | collective-permute-done | bytes 8388640 | tf_op jit(solution)/shard_map/ppermute | solution.py:70
  49.3 11.1 %add.69 = f32[4,2,512,512]{3,2,1,0:T(8,128)} add(f32[4,2,512,512]{3,2,1,0:T(8,128)} %copy-done.2, f32[4,2,512,512]{3,2,1,0:T(8,128)} %collective-permute-done) | non-fusion elementwise | flops 2097152 | bytes 25165824 | tf_op jit(solution)/shard_map/add | solution.py:70
  60.4 1.6 collective-permute-start.1
  61.9 181.2 %collective-permute-done.1 = f32[4,2,512,512]{3,2,1,0:T(8,128)} collective-permute-done((f32[4,2,512,512]{3,2,1,0:T(8,128)}, f32[4,2,512,512]{3,2,1,0:T(8,128)}, u32[]{:S(2)}, u32[]{:S(2)}) %collective-permute-start.1) | collective-permute-done | bytes 8388640 | tf_op jit(solution)/shard_map/ppermute | solution.py:70
  243.2 11.1 %add.70 = f32[4,2,512,512]{3,2,1,0:T(8,128)} add(f32[4,2,512,512]{3,2,1,0:T(8,128)} %add.69, f32[4,2,512,512]{3,2,1,0:T(8,128)} %collective-permute-done.1) | non-fusion elementwise | flops 2097152 | bytes 25165824 | tf_op jit(solution)/shard_map/add | solution.py:70
  254.3 1.6 collective-permute-start.2
  255.9 180.3 %collective-permute-done.2 = f32[4,2,512,512]{3,2,1,0:T(8,128)} collective-permute-done((f32[4,2,512,512]{3,2,1,0:T(8,128)}, f32[4,2,512,512]{3,2,1,0:T(8,128)}, u32[]{:S(2)}, u32[]{:S(2)}) %collective-permute-start.2) | collective-permute-done | bytes 8388640 | tf_op jit(solution)/shard_map/ppermute | solution.py:70
  436.2 11.1 %add.71 = f32[4,2,512,512]{3,2,1,0:T(8,128)} add(f32[4,2,512,512]{3,2,1,0:T(8,128)} %add.70, f32[4,2,512,512]{3,2,1,0:T(8,128)} %collective-permute-done.2) | non-fusion elementwise | flops 2097152 | bytes 25165824 | tf_op jit(solution)/shard_map/add | solution.py:70
  447.3 2.7 collective-permute-start.3
  450.2 358.9 %collective-permute-done.3 = f32[4,2,512,512]{3,2,1,0:T(8,128)} collective-permute-done((f32[4,2,512,512]{3,2,1,0:T(8,128)}, f32[4,2,512,512]{3,2,1,0:T(8,128)}, u32[]{:S(2)}, u32[]{:S(2)}) %collective-permute-start.3) | collective-permute-done | bytes 8388640 | tf_op jit(solution)/shard_map/ppermute | solution.py:70
  809.1 10.4 %abs_reduce_fusion = (f32[4,2,512]{2,1,0:T(2,128)S(1)}, f32[4,2,512,512]{3,2,1,0:T(8,128)}) fusion(f32[512,512]{1,0:T(8,128)S(1)} %fusion.10, f32[4,2]{1,0:T(4,128)S(1)} %copy.43, f32[4,2,512,512]{3,2,1,0:T(8,128)} %add.71, f32[4,2,512,512]{3,2,1,0:T(8,128)} %collective-permute-done.3), kind=kLoop, calls=%fused_computation.6 | loop fusion | flops 10481664 | bytes 26230816 | tf_op jit(solution)/shard_map/reduce_sum | solution.py:72
  819.9 22.2 %fusion.1 = f32[4,2,512,512]{3,2,1,0:T(8,128)} fusion(f32[4,2,512,512]{3,2,1,0:T(8,128)} %get-tuple-element.3, f32[4,2]{1,0:T(4,128)S(1)} %copy.46, f32[4,2]{1,0:T(4,128)S(1)} %copy.45, f32[512,512]{1,0:T(8,128)S(1)} %fusion.10), kind=kOutput, calls=%fused_computation.5 | convolution fusion | flops 12891193344 | bytes 17825856 | tf_op jit(solution)/shard_map/eirk,eikc->eirc/dot_general | solution.py:27
  842.1 19.2 %multiply_subtract_fusion = f32[4,2,512,512]{3,2,1,0:T(8,128)} fusion(f32[4,2,512,512]{3,2,1,0:T(8,128)S(1)} %copy-done, f32[4,2,512,512]{3,2,1,0:T(8,128)} %fusion.1, f32[4,2]{1,0:T(4,128)S(1)} %copy.46, f32[4,2]{1,0:T(4,128)S(1)} %copy.45, f32[512,512]{1,0:T(8,128)S(1)} %fusion.10), kind=kOutput, calls=%fused_computation.2 | convolution fusion | flops 12901679104 | bytes 26214464 | tf_op jit(solution)/shard_map/eirk,eikc->eirc/dot_general | solution.py:28
  861.3 6.0 fusion.12
  867.3 4.9 multiply_subtract_fusion.6
  872.3 7.8 all_gather.6
  880.1 7.0 all_gather.7
  887.1 0.8 copy.52
  887.9 0.8 copy.53
  (45 shorter events, 3.8 us)
Async XLA Ops:
  32.8 3.2 copy-start.2
  36.0 13.3 %collective-permute-start = (f32[4,2,512,512]{3,2,1,0:T(8,128)S(1)}, f32[4,2,512,512]{3,2,1,0:T(8,128)}, u32[]{:S(2)}, u32[]{:S(2)}) collective-permute-start(f32[4,2,512,512]{3,2,1,0:T(8,128)S(1)} %broadcast_multiply_fusion), channel_id=1, source_target_pairs={{0,1},{1,0},{2,3},{3,2},{4,5},{5,4},{6,7},{7,6},{8,9},{9,8},{10,11... | collective-permute-start | bytes 25165832 | tf_op jit(solution)/shard_map/ppermute | solution.py:70
  60.4 182.8 %collective-permute-start.1 = (f32[4,2,512,512]{3,2,1,0:T(8,128)}, f32[4,2,512,512]{3,2,1,0:T(8,128)}, u32[]{:S(2)}, u32[]{:S(2)}) collective-permute-start(f32[4,2,512,512]{3,2,1,0:T(8,128)} %add.69), channel_id=1, source_target_pairs={{0,2},{1,3},{2,0},{3,1},{4,6},{5,7},{6,4},{7,5},{8,10},{9,11},{10,... | collective-permute-start | bytes 25165832 | tf_op jit(solution)/shard_map/ppermute | solution.py:70
  254.3 195.7 %copy-start.3 = (f32[4,2,1]{0,2,1:T(1,128)S(1)}, f32[4,2,1]{0,2,1:T(1,128)}, u32[]{:S(2)}) copy-start(f32[4,2,1]{0,2,1:T(1,128)} %param.11) | copy-start | bytes 100
  254.3 182.0 %collective-permute-start.2 = (f32[4,2,512,512]{3,2,1,0:T(8,128)}, f32[4,2,512,512]{3,2,1,0:T(8,128)}, u32[]{:S(2)}, u32[]{:S(2)}) collective-permute-start(f32[4,2,512,512]{3,2,1,0:T(8,128)} %add.70), channel_id=1, source_target_pairs={{0,4},{1,5},{2,6},{3,7},{4,0},{5,1},{6,2},{7,3},{8,12},{9,13},{10,... | collective-permute-start | bytes 25165832 | tf_op jit(solution)/shard_map/ppermute | solution.py:70
  447.3 361.8 %collective-permute-start.3 = (f32[4,2,512,512]{3,2,1,0:T(8,128)}, f32[4,2,512,512]{3,2,1,0:T(8,128)}, u32[]{:S(2)}, u32[]{:S(2)}) collective-permute-start(f32[4,2,512,512]{3,2,1,0:T(8,128)} %add.71), channel_id=1, source_target_pairs={{0,8},{1,9},{2,10},{3,11},{4,12},{5,13},{6,14},{7,15},{8,0},{9,1},... | collective-permute-start | bytes 25165832 | tf_op jit(solution)/shard_map/ppermute | solution.py:70
  819.9 22.2 %copy-start = (f32[4,2,512,512]{3,2,1,0:T(8,128)S(1)}, f32[4,2,512,512]{3,2,1,0:T(8,128)}, u32[]{:S(2)}) copy-start(f32[4,2,512,512]{3,2,1,0:T(8,128)} %get-tuple-element.3) | copy-start | bytes 25165828
  861.3 6.1 copy-start.1
